TPU v7x, 32 devices: a whole 2x2x4 slice. The times are simulated.
32 devices in a mesh: row: 8 (over y, x, core), col: 4 (over z).
Axes of the slice: x: 2, y: 2, z: 4, core: 2. Of those that a mesh axis runs over, the one named last changes fastest.
Arguments:
- rho_real: float32 [8192, 8192], P('row', 'col'), may hold values from -6 to 12, as said below
- rho_imag: float32 [8192, 8192], P('row', 'col'), may hold values from -6 to 6, as said below
- gate_real_matrix: float32 [16, 16], replicated, may hold values from -1 to 1, as said below
- gate_imaginary: float32 [16, 16], replicated, may hold values from -1 to 1, as said below
- angles: float32 [8, 3], replicated, may hold values from -3.140625 to 3.140625
- targets: int32 [8], replicated, may hold values from 0 to 4
- gate_order: int32 [8], replicated, may hold values from 0 to 7, each once
Outputs:
- mixed_real: float32 [8192, 8192], P('row', 'col')
- depolarized_quadrature: float32 [8192, 8192], P('row', 'col')
- purity: float32 [], replicated
Inputs may be any that keep to these rules, and one draw needn't show every extreme that they name: rho_real is symmetric: entries of order one off the diagonal, each diagonal entry raised by 2 to 6. rho_imag is antisymmetric with a zero diagonal, so that rho_real + i rho_imag is Hermitian. gate_real_matrix + i gate_imaginary is a unitary matrix. gate_real_matrix + i gate_imaginary is a unitary matrix. `targets`: each gate acts on one of the 5 low qubits. `gate_order`: each gate appears once.
All inputs are finite; a program needn't handle non-finite values.
Results may differ from a plain program's by a relative error of at most 0.0001.
Values sent between devices are 32-bit elements; how exact they have to be, the bound alone decides.
A program may use at most 128 MiB of HBM per device.

v0:
```python
import jax
import jax.numpy as jnp
from jax import lax
from jax.sharding import PartitionSpec as P

LQ = 5
GATE = 16
DIM = 8192


highest = lax.Precision.HIGHEST
mixing = 0.25


def complex_blend(pattern, left_real, left_imag, right_real, right_imag):
    real_part = jnp.einsum(pattern, left_real, right_real, precision=highest) - jnp.einsum(
        pattern, left_imag, right_imag, precision=highest
    )
    imag_part = jnp.einsum(pattern, left_real, right_imag, precision=highest) + jnp.einsum(
        pattern, left_imag, right_real, precision=highest
    )
    return (real_part, imag_part)


def embed_gate(angle_row, target, low_width):
    half_turn = angle_row[0] / 2
    cosine_half = jnp.cos(half_turn)
    sine_half = jnp.sin(half_turn)
    phase_first = angle_row[1]
    phase_second = angle_row[2]
    element_count = (
        (cosine_half, cosine_half * 0.0),
        (-jnp.cos(phase_second) * sine_half, -jnp.sin(phase_second) * sine_half),
        (jnp.cos(phase_first) * sine_half, jnp.sin(phase_first) * sine_half),
        (
            jnp.cos(phase_first + phase_second) * cosine_half,
            jnp.sin(phase_first + phase_second) * cosine_half,
        ),
    )
    left_index = lax.broadcasted_iota(jnp.int32, (low_width, low_width), 0)
    right_index = lax.broadcasted_iota(jnp.int32, (low_width, low_width), 1)
    target_bit = jnp.left_shift(jnp.ones((), jnp.int32), target)
    same_rest = jnp.bitwise_or(jnp.bitwise_xor(left_index, right_index), target_bit) == target_bit
    left_high = jnp.bitwise_and(left_index, target_bit) > 0
    right_high = jnp.bitwise_and(right_index, target_bit) > 0
    result = []
    for member in range(2):
        chosen = jnp.where(
            left_high,
            jnp.where(right_high, element_count[3][member], element_count[2][member]),
            jnp.where(right_high, element_count[1][member], element_count[0][member]),
        )
        result.append(jnp.where(same_rest, chosen, jnp.zeros_like(chosen)))
    return (result[0], result[1])


def joined_gate(angles, targets, gate_order, low_width):
    gate_count = angles.shape[0]
    slot_ids = jnp.arange(gate_count, dtype=jnp.int32)
    total_real = jnp.eye(low_width, dtype=jnp.float32)
    total_imag = jnp.zeros((low_width, low_width), jnp.float32)
    for position in range(gate_count):
        picked = slot_ids == gate_order[position]
        angle_row = jnp.sum(jnp.where(picked[:, None], angles, jnp.zeros_like(angles)), axis=0)
        target = jnp.sum(jnp.where(picked, targets, jnp.zeros_like(targets)))
        step_real, step_imag = embed_gate(angle_row, target, low_width)
        total_real, total_imag = complex_blend(
            "ab,bc->ac", step_real, step_imag, total_real, total_imag
        )
    return (total_real, total_imag)


def on_device(rho_real, rho_imag, gate_real_matrix, gate_imaginary, angles, targets, gate_order):
    row_count, col_count = rho_real.shape
    low_width = 2**LQ
    row_parts = GATE // lax.axis_size("row")
    col_parts = GATE // lax.axis_size("col")
    block_inphase_component, block_quadrature = joined_gate(angles, targets, gate_order, low_width)
    moved = (
        lax.all_to_all(
            rho_real.reshape(row_parts, GATE, low_width * col_count),
            "row",
            split_axis=1,
            concat_axis=0,
            tiled=True,
        ),
        lax.all_to_all(
            rho_imag.reshape(row_parts, GATE, low_width * col_count),
            "row",
            split_axis=1,
            concat_axis=0,
            tiled=True,
        ),
    )
    center_divide = complex_blend(
        "sx,xazw->aszw",
        gate_real_matrix,
        gate_imaginary,
        moved[0].reshape(GATE, row_parts, low_width, col_count),
        moved[1].reshape(GATE, row_parts, low_width, col_count),
    )
    rotated_state = complex_blend(
        "us,ebsl->ebul",
        block_inphase_component,
        block_quadrature,
        center_divide[0],
        center_divide[1],
    )
    moved = (
        lax.all_to_all(
            rotated_state[0].reshape(row_count, col_parts, GATE * low_width),
            "col",
            split_axis=2,
            concat_axis=1,
            tiled=True,
        ),
        lax.all_to_all(
            rotated_state[1].reshape(row_count, col_parts, GATE * low_width),
            "col",
            split_axis=2,
            concat_axis=1,
            tiled=True,
        ),
    )
    center_divide = complex_blend(
        "rghl,Gg->rhGl",
        moved[0].reshape(row_count, GATE, col_parts, low_width),
        moved[1].reshape(row_count, GATE, col_parts, low_width),
        gate_real_matrix,
        -gate_imaginary,
    )
    final = complex_blend(
        "rhGl,Ll->rhGL",
        center_divide[0],
        center_divide[1],
        block_inphase_component,
        -block_quadrature,
    )
    new_real = final[0].reshape(row_count, col_count)
    updated_quadrature = final[1].reshape(row_count, col_count)
    row_global = lax.axis_index("row") * row_count + lax.broadcasted_iota(
        jnp.int32, (row_count, col_count), 0
    )
    col_global = lax.axis_index("col") * col_count + lax.broadcasted_iota(
        jnp.int32, (row_count, col_count), 1
    )
    diagonal = row_global == col_global
    part_trace_real = jnp.sum(jnp.where(diagonal, new_real, jnp.zeros_like(new_real)))
    part_trace_imag = jnp.sum(
        jnp.where(diagonal, updated_quadrature, jnp.zeros_like(updated_quadrature))
    )
    keep_share = 1 - mixing
    part_squares = jnp.sum(new_real * new_real) + jnp.sum(updated_quadrature * updated_quadrature)
    trace_real, trace_imag, squares = lax.psum(
        (part_trace_real, part_trace_imag, part_squares), ("row", "col")
    )
    shift_real = mixing * trace_real / DIM
    shift_imag = mixing * trace_imag / DIM
    mixed_real = keep_share * new_real + jnp.where(diagonal, shift_real, jnp.zeros_like(new_real))
    depolarized_quadrature = keep_share * updated_quadrature + jnp.where(
        diagonal, shift_imag, jnp.zeros_like(updated_quadrature)
    )
    trace_squared = trace_real * trace_real + trace_imag * trace_imag
    purity = (
        keep_share * keep_share * squares
        + (2 * keep_share * mixing + mixing * mixing) * trace_squared / DIM
    ) / (DIM * DIM)
    return (mixed_real, depolarized_quadrature, purity)


def solution(mesh):
    in_specs = (P("row", "col"), P("row", "col"), P(), P(), P(), P(), P())
    out_specs = (P("row", "col"), P("row", "col"), P())
    return jax.shard_map(
        on_device, mesh=mesh, in_specs=in_specs, out_specs=out_specs, check_vma=False
    )
```

profile of v0, /device:TPU:14, one launch (start us, length us, event | category | flops | bytes accessed | tf_op | source)
XLA Modules:
  0.0 953.0 jit_solution(4701078371435506162)
XLA Ops:
  0.6 7.5 reshape.225
  8.2 15.4 %copy.80 = f32[2,16,65536]{2,0,1:T(2,128)} copy(f32[2,16,65536]{2,1,0:T(8,128)} %reshape.225) | data formatting | bytes 16777216 | tf_op jit(solution)/shard_map/reshape | solution.py:81
  23.6 5.5 all-to-all-start
  29.1 0.7 fusion.245
  29.7 0.6 iota_compare_fusion.4
  30.4 0.7 iota_compare_fusion.5
  31.1 0.7 iota_compare_fusion.6
  31.7 0.6 iota_compare_fusion.7
  32.3 0.6 iota_compare_fusion.8
  32.9 0.6 iota_compare_fusion.9
  33.6 0.6 iota_compare_fusion.10
  34.2 0.7 iota_compare_fusion.3
  34.9 0.2 select_reduce_fusion.7
  35.1 0.7 fusion.237
  45.8 0.7 fusion.241
  56.4 0.6 fusion.239
  66.7 0.7 fusion.243
  76.1 5.9 select_reduce_fusion.15
  87.2 7.5 reshape.227
  94.7 15.3 %copy.83 = f32[2,16,65536]{2,0,1:T(2,128)} copy(f32[2,16,65536]{2,1,0:T(8,128)} %reshape.227) | data formatting | bytes 16777216 | tf_op jit(solution)/shard_map/reshape | solution.py:88
  110.6 10.3 %all-to-all-done = f32[2,16,65536]{2,0,1:T(2,128)} async-done(((f32[2,16,65536]{2,0,1:T(2,128)}), f32[2,16,65536]{2,0,1:T(2,128)}, u32[]{:S(2)}, u32[]{:S(2)}) %all-to-all-start) | async-done | bytes 8388640 | tf_op jit(solution)/shard_map/all_to_all | solution.py:80
  120.9 7.9 all-to-all-start.1
  130.9 0.2 convolution_subtract_fusion.7
  131.5 0.2 convolution_add_fusion.6
  132.0 0.2 convolution_subtract_fusion.6
  133.7 0.2 convolution_subtract_fusion.4
  135.9 0.2 convolution_subtract_fusion.1
  137.2 15.3 %copy.81 = f32[8,2,2,65536]{3,2,1,0:T(2,128)} copy(f32[8,2,2,65536]{3,1,2,0:T(2,128)} %bitcast.1) | data formatting | bytes 16777216 | tf_op jit(solution)/shard_map/all_to_all | solution.py:80
  152.5 15.0 %reshape.226 = f32[16,2,32,2048]{3,2,1,0:T(8,128)} reshape(f32[8,2,2,65536]{3,2,1,0:T(2,128)} %copy.81) | data formatting | bytes 16777216 | tf_op jit(solution)/shard_map/reshape | solution.py:99
  167.5 53.0 %all-to-all-done.1 = f32[2,16,65536]{2,0,1:T(2,128)} async-done(((f32[2,16,65536]{2,0,1:T(2,128)}), f32[2,16,65536]{2,0,1:T(2,128)}, u32[]{:S(2)}, u32[]{:S(2)}) %all-to-all-start.1) | async-done | bytes 8388640 | tf_op jit(solution)/shard_map/all_to_all | solution.py:87
  220.5 15.3 %copy.84 = f32[8,2,2,65536]{3,2,1,0:T(2,128)} copy(f32[8,2,2,65536]{3,1,2,0:T(2,128)} %bitcast.5) | data formatting | bytes 16777216 | tf_op jit(solution)/shard_map/all_to_all | solution.py:87
  235.8 15.0 %reshape.228 = f32[16,2,32,2048]{3,2,1,0:T(8,128)} reshape(f32[8,2,2,65536]{3,2,1,0:T(2,128)} %copy.84) | data formatting | bytes 16777216 | tf_op jit(solution)/shard_map/reshape | solution.py:100
  250.8 18.8 %fusion.20 = f32[2,32,2048,16]{2,3,1,0:T(8,128)S(1)} fusion(f32[16,2,32,2048]{3,2,1,0:T(8,128)} %reshape.228, f32[16,16]{1,0:T(8,128)S(1)} %copy-done), kind=kOutput, calls=%fused_computation.34 | convolution fusion | flops 402653184 | bytes 16778240 | tf_op jit(solution)/shard_map/sx,xazw->aszw/dot_general | solution.py:19
  269.6 16.3 %fusion.22 = f32[2,32,2048,16]{2,3,1,0:T(8,128)} fusion(f32[16,2,32,2048]{3,2,1,0:T(8,128)S(1)} %copy-done.3, f32[16,16]{1,0:T(8,128)S(1)} %copy-done.6), kind=kOutput, calls=%fused_computation.36 | convolution fusion | flops 402653184 | bytes 16778240 | tf_op jit(solution)/shard_map/sx,xazw->aszw/dot_general | solution.py:16
  285.9 19.8 %add_bitcast_fusion.2 = f32[2,16,32,2048]{3,1,2,0:T(8,128)S(1)} fusion(f32[2,32,2048,16]{2,3,1,0:T(8,128)S(1)} %fusion.20, f32[16,2,32,2048]{3,2,1,0:T(8,128)} %reshape.226, f32[16,16]{1,0:T(8,128)S(1)} %copy-done.6), kind=kOutput, calls=%fused_computation.16 | convolution fusion | flops 404750336 | bytes 25166848 | tf_op jit(solution)/shard_map/sx,xazw->aszw/dot_general | solution.py:19
  305.8 20.5 %subtract_bitcast_fusion.2 = f32[2,16,32,2048]{3,1,2,0:T(8,128)S(1)} fusion(f32[2,32,2048,16]{2,3,1,0:T(8,128)} %fusion.22, f32[16,2,32,2048]{3,2,1,0:T(8,128)S(1)} %bitcast.184, f32[16,16]{1,0:T(8,128)S(1)} %copy-done), kind=kOutput, calls=%fused_computation.17 | convolution fusion | flops 404750336 | bytes 25166848 | tf_op jit(solution)/shard_map/sx,xazw->aszw/dot_general | solution.py:16
  326.3 17.0 %fusion.14 = f32[2,16,2048,32]{2,3,1,0:T(8,128)S(1)} fusion(f32[2,16,32,2048]{3,1,2,0:T(8,128)S(1)} %add_bitcast_fusion.2, f32[32,32]{1,0:T(8,128)S(1)} %convolution_add_fusion), kind=kOutput, calls=%fused_computation.28 | convolution fusion | flops 805306368 | bytes 16781312 | tf_op jit(solution)/shard_map/us,ebsl->ebul/dot_general | solution.py:16
  343.3 17.8 %subtract_bitcast_fusion.1 = f32[2,16,32,2048]{3,2,1,0:T(8,128)} fusion(f32[2,16,2048,32]{2,3,1,0:T(8,128)S(1)} %fusion.14, f32[32,32,1,1]{1,0,3,2:T(8,128)S(1)} %fusion.42, f32[2,16,32,2048]{3,1,2,0:T(8,128)S(1)} %subtract_bitcast_fusion.2), kind=kOutput, calls=%fused_computation.15 | convolution fusion | flops 807403520 | bytes 25169920 | tf_op jit(solution)/shard_map/us,ebsl->ebul/dot_general | solution.py:16
  361.2 10.8 %reshape.229 = f32[1024,4,512]{2,1,0:T(4,128)} reshape(f32[2,16,32,2048]{3,2,1,0:T(8,128)} %subtract_bitcast_fusion.1) | data formatting | bytes 16777216 | tf_op jit(solution)/shard_map/reshape | solution.py:111
  372.0 11.3 %copy.90 = f32[1024,4,512]{0,1,2:T(4,128)} copy(f32[1024,4,512]{2,1,0:T(4,128)} %reshape.229) | data formatting | bytes 16777216 | tf_op jit(solution)/shard_map/reshape | solution.py:111
  383.3 5.8 all-to-all-start.2
  389.1 18.8 %fusion.12 = f32[2,16,2048,32]{2,3,1,0:T(8,128)S(1)} fusion(f32[32,32,1,1]{1,0,3,2:T(8,128)S(1)} %fusion.42, f32[2,16,32,2048]{3,1,2,0:T(8,128)} %copy-done.2), kind=kOutput, calls=%fused_computation.26 | convolution fusion | flops 805306368 | bytes 16781312 | tf_op jit(solution)/shard_map/us,ebsl->ebul/dot_general | solution.py:19
  408.0 22.4 %add_bitcast_fusion.1 = f32[2,16,32,2048]{3,2,1,0:T(8,128)} fusion(f32[2,16,2048,32]{2,3,1,0:T(8,128)S(1)} %fusion.12, f32[2,16,32,2048]{3,1,2,0:T(8,128)} %copy-done.4, f32[32,32]{1,0:T(8,128)S(1)} %convolution_add_fusion), kind=kOutput, calls=%fused_computation.14 | convolution fusion | flops 807403520 | bytes 25169920 | tf_op jit(solution)/shard_map/us,ebsl->ebul/dot_general | solution.py:19
  430.4 10.8 %reshape.231 = f32[1024,4,512]{2,1,0:T(4,128)} reshape(f32[2,16,32,2048]{3,2,1,0:T(8,128)} %add_bitcast_fusion.1) | data formatting | bytes 16777216 | tf_op jit(solution)/shard_map/reshape | solution.py:118
  441.2 11.4 %copy.94 = f32[1024,4,512]{0,1,2:T(4,128)} copy(f32[1024,4,512]{2,1,0:T(4,128)} %reshape.231) | data formatting | bytes 16777216 | tf_op jit(solution)/shard_map/reshape | solution.py:118
  452.6 116.7 %all-to-all-done.2 = f32[1024,4,512]{0,1,2:T(4,128)} async-done(((f32[1024,4,512]{0,1,2:T(4,128)}), f32[1024,4,512]{0,1,2:T(4,128)}, u32[]{:S(2)}, u32[]{:S(2)}) %all-to-all-start.2) | async-done | bytes 8388640 | tf_op jit(solution)/shard_map/all_to_all | solution.py:110
  569.4 9.3 all-to-all-start.3
  578.8 9.8 %copy.149 = f32[1024,4,4,128]{0,1,2,3:T(4,128)} copy(f32[1024,4,4,128]{0,1,3,2:T(4,128)} %bitcast.81) | data formatting | bytes 16777216 | tf_op jit(solution)/shard_map/all_to_all | solution.py:110
  588.6 10.0 %reshape.230 = f32[1024,16,4,32]{0,1,3,2:T(8,128)} reshape(f32[1024,4,4,128]{0,2,1,3:T(4,128)} %bitcast.187) | data formatting | bytes 16777216 | tf_op jit(solution)/shard_map/reshape | solution.py:127
  598.5 12.9 %fusion.65 = f32[1024,4,32,16]{0,3,2,1:T(8,128)} fusion(f32[1024,16,4,32]{0,1,3,2:T(8,128)} %reshape.230, f32[16,16]{1,0:T(8,128)S(1)} %copy-done.6), kind=kOutput, calls=%fused_computation.112 | convolution fusion | flops 402653440 | bytes 16778240 | tf_op jit(solution)/shard_map/rghl,Gg->rhGl/dot_general | solution.py:19
  611.4 11.0 %fusion.71 = f32[1024,4,32,16]{0,3,2,1:T(8,128)} fusion(f32[1024,16,4,32]{0,1,3,2:T(8,128)S(1)} %copy-done.1, f32[16,16]{1,0:T(8,128)S(1)} %copy-done), kind=kOutput, calls=%fused_computation.118 | convolution fusion | flops 402653184 | bytes 16778240 | tf_op jit(solution)/shard_map/rghl,Gg->rhGl/dot_general | solution.py:16
  622.4 135.7 %all-to-all-done.3 = f32[1024,4,512]{0,1,2:T(4,128)} async-done(((f32[1024,4,512]{0,1,2:T(4,128)}), f32[1024,4,512]{0,1,2:T(4,128)}, u32[]{:S(2)}, u32[]{:S(2)}) %all-to-all-start.3) | async-done | bytes 8388640 | tf_op jit(solution)/shard_map/all_to_all | solution.py:117
  758.1 9.8 %copy.148 = f32[1024,4,4,128]{0,1,2,3:T(4,128)} copy(f32[1024,4,4,128]{0,1,3,2:T(4,128)} %bitcast.86) | data formatting | bytes 16777216 | tf_op jit(solution)/shard_map/all_to_all | solution.py:117
  767.9 10.0 %reshape.232 = f32[1024,16,4,32]{0,1,3,2:T(8,128)} reshape(f32[1024,4,4,128]{0,2,1,3:T(4,128)} %bitcast.188) | data formatting | bytes 16777216 | tf_op jit(solution)/shard_map/reshape | solution.py:128
  777.9 15.5 %add_bitcast_fusion = f32[1024,4,16,32]{0,2,3,1:T(8,128)S(1)} fusion(f32[1024,4,32,16]{0,3,2,1:T(8,128)} %fusion.65, f32[1024,16,4,32]{0,1,3,2:T(8,128)} %reshape.232, f32[16,16]{1,0:T(8,128)S(1)} %copy-done), kind=kOutput, calls=%fused_computation.12 | convolution fusion | flops 404750336 | bytes 25166848 | tf_op jit(solution)/shard_map/rghl,Gg->rhGl/dot_general | solution.py:19
  793.4 15.1 %fusion.4 = f32[1024,4,16,32]{0,3,2,1:T(8,128)} fusion(f32[32,32,1,1]{1,0,3,2:T(8,128)S(1)} %fusion.42, f32[1024,4,16,32]{0,2,3,1:T(8,128)S(1)} %add_bitcast_fusion), kind=kOutput, calls=%fused_computation.18 | convolution fusion | flops 805306368 | bytes 16781312 | tf_op jit(solution)/shard_map/rhGl,Ll->rhGL/dot_general | solution.py:19
  808.5 14.7 %fusion.6 = f32[1024,4,16,32]{0,3,2,1:T(8,128)} fusion(f32[1024,4,16,32]{0,2,3,1:T(8,128)S(1)} %add_bitcast_fusion, f32[32,32]{1,0:T(8,128)S(1)} %convolution_add_fusion), kind=kOutput, calls=%fused_computation.20 | convolution fusion | flops 805307392 | bytes 16781312 | tf_op jit(solution)/shard_map/rhGl,Ll->rhGL/dot_general | solution.py:16
  823.2 13.9 %subtract_bitcast_fusion = f32[1024,4,16,32]{0,2,3,1:T(8,128)S(1)} fusion(f32[1024,4,32,16]{0,3,2,1:T(8,128)} %fusion.71, f32[1024,16,4,32]{0,1,3,2:T(8,128)S(1)} %bitcast.182, f32[16,16]{1,0:T(8,128)S(1)} %copy-done.6), kind=kOutput, calls=%fused_computation.13 | convolution fusion | flops 404750592 | bytes 25166848 | tf_op jit(solution)/shard_map/rghl,Gg->rhGl/dot_general | solution.py:16
  837.1 15.3 %fusion.36 = f32[1024,4,16,32]{0,3,2,1:T(8,128)} fusion(f32[1024,4,16,32]{0,3,2,1:T(8,128)S(1)} %copy-done.5, f32[32,32,1,1]{1,0,3,2:T(8,128)S(1)} %fusion.42, f32[1024,4,16,32]{0,2,3,1:T(8,128)S(1)} %subtract_bitcast_fusion), kind=kOutput, calls=%fused_computation.44 | convolution fusion | flops 807403520 | bytes 25169920 | tf_op jit(solution)/shard_map/rhGl,Ll->rhGL/dot_general | solution.py:16
  852.4 19.9 %multiply_reduce_fusion = (f32[]{:T(128)}, f32[]{:T(128)}, f32[1024,4,16,32]{0,3,2,1:T(8,128)}, f32[1024,4,16,32]{0,3,2,1:T(8,128)}, f32[]{:T(128)}, /*index=5*/f32[]{:T(128)}) fusion(s32[4,16,32]{2,1,0:T(8,128)S(1)} %add_add_fusion, s32[1024]{0:T(1024)S(1)} %iota_add_fusion.1, f32[1024,4,16,32]{0,3,2,1:T(8,128)} %fusion.36, ...), kind=kOutput, calls=%fused_computation.10 | convolution fusion | flops 830473216 | bytes 41959440 | tf_op jit(solution)/shard_map/rhGl,Ll->rhGL/dot_general | solution.py:19
  873.7 43.8 %all-reduce = (f32[]{:T(128)}, f32[]{:T(128)}, f32[]{:T(128)}) all-reduce(f32[]{:T(128)} %get-tuple-element.29, f32[]{:T(128)} %get-tuple-element.4, f32[]{:T(128)S(6)} %add.158), channel_id=1, replica_groups=mesh['row'=8,'col'=4] {'row','col'}, use_global_device_ids=true, to_apply=%region_17.18 | all-reduce | flops 3 | bytes 24 | tf_op jit(solution)/shard_map/psum | solution.py:154
  921.3 9.2 copy.101
  930.5 9.1 copy.98
  940.2 11.5 %fusion.1 = (f32[1024,2048]{1,0:T(8,128)}, f32[1024,2048]{1,0:T(8,128)}) fusion(f32[1024,2048]{1,0:T(8,128)} %copy.101, f32[]{:T(128)S(6)} %div.45, s32[2048]{0:T(1024)S(1)} %iota_add_fusion, s32[1024]{0:T(1024)S(1)} %iota_add_fusion.1, f32[1024,2048]{1,0:T(8,128)} %copy.98, f32[]{:T(128)S(6)} %div.44), kind=kLoop, calls=%fused_computation.5 | loop fusion | flops 10485760 | bytes 33566728 | tf_op jit(solution)/shard_map/add | solution.py:160
  (100 shorter events, 6.1 us)
Async XLA Ops:
  0.6 250.1 %copy-start = (f32[16,16]{1,0:T(8,128)S(1)}, f32[16,16]{1,0:T(8,128)}, u32[]{:S(2)}) copy-start(f32[16,16]{1,0:T(8,128)} %param.9) | copy-start | bytes 3076
  23.6 5.5 copy-start.7
  23.6 11.3 %copy-start.8 = (f32[8,3]{0,1:T(4,128)S(1)}, f32[8,3]{0,1:T(4,128)}, u32[]{:S(2)}) copy-start(f32[8,3]{0,1:T(4,128)} %param.11) | copy-start | bytes 292
  23.6 52.5 %copy-start.9 = (s32[8]{0:T(128)S(1)}, s32[8]{0:T(128)}, u32[]{:S(2)}) copy-start(s32[8]{0:T(128)} %param.12) | copy-start | bytes 100
  23.6 97.3 %all-to-all-start = ((f32[2,16,65536]{2,0,1:T(2,128)}), f32[2,16,65536]{2,0,1:T(2,128)}, u32[]{:S(2)}, u32[]{:S(2)}) async-start(f32[2,16,65536]{2,0,1:T(2,128)} %copy.80), calls=%async_computation | async-start | bytes 16777216 | tf_op jit(solution)/shard_map/all_to_all | solution.py:80
  120.9 99.6 %all-to-all-start.1 = ((f32[2,16,65536]{2,0,1:T(2,128)}), f32[2,16,65536]{2,0,1:T(2,128)}, u32[]{:S(2)}, u32[]{:S(2)}) async-start(f32[2,16,65536]{2,0,1:T(2,128)} %copy.83), calls=%async_computation.1 | async-start | bytes 16777216 | tf_op jit(solution)/shard_map/all_to_all | solution.py:87
  250.8 18.8 %copy-start.3 = (f32[16,2,32,2048]{3,2,1,0:T(8,128)S(1)}, f32[16,2,32,2048]{3,2,1,0:T(8,128)}, u32[]{:S(2)}) copy-start(f32[16,2,32,2048]{3,2,1,0:T(8,128)} %reshape.228) | copy-start | bytes 25165828
  250.8 18.8 %copy-start.6 = (f32[16,16]{1,0:T(8,128)S(1)}, f32[16,16]{1,0:T(8,128)}, u32[]{:S(2)}) copy-start(f32[16,16]{1,0:T(8,128)} %param.10) | copy-start | bytes 3076
  269.6 36.2 %slice-start.2 = ((s8[8388608]{0:T(1024)(128)(4,1)}), s8[4194304]{0:T(1024)(128)(4,1)S(1)}, s32[]{:S(2)}) async-start(s8[8388608]{0:T(1024)(128)(4,1)} %bitcast.183), calls=%async_computation.6 | async-start | bytes 8388608
  285.9 19.8 %slice-start.3 = ((s8[8388608]{0:T(1024)(128)(4,1)}), s8[4194304]{0:T(1024)(128)(4,1)S(1)}, s32[]{:S(2)}) async-start(s8[8388608]{0:T(1024)(128)(4,1)} %bitcast.183), calls=%async_computation.7 | async-start | bytes 8388608
  305.8 20.5 %copy-start.2 = (f32[2,16,32,2048]{3,1,2,0:T(8,128)}, f32[2,16,32,2048]{3,1,2,0:T(8,128)S(1)}, u32[]{:S(2)}) copy-start(f32[2,16,32,2048]{3,1,2,0:T(8,128)S(1)} %add_bitcast_fusion.2) | copy-start | bytes 25165828
  326.3 17.0 %copy-start.4 = (f32[2,16,32,2048]{3,1,2,0:T(8,128)}, f32[2,16,32,2048]{3,1,2,0:T(8,128)S(1)}, u32[]{:S(2)}) copy-start(f32[2,16,32,2048]{3,1,2,0:T(8,128)S(1)} %subtract_bitcast_fusion.2) | copy-start | bytes 25165828
  383.3 186.1 %all-to-all-start.2 = ((f32[1024,4,512]{0,1,2:T(4,128)}), f32[1024,4,512]{0,1,2:T(4,128)}, u32[]{:S(2)}, u32[]{:S(2)}) async-start(f32[1024,4,512]{0,1,2:T(4,128)} %copy.90), calls=%async_computation.2 | async-start | bytes 16777216 | tf_op jit(solution)/shard_map/all_to_all | solution.py:110
  569.4 188.7 %all-to-all-start.3 = ((f32[1024,4,512]{0,1,2:T(4,128)}), f32[1024,4,512]{0,1,2:T(4,128)}, u32[]{:S(2)}, u32[]{:S(2)}) async-start(f32[1024,4,512]{0,1,2:T(4,128)} %copy.94), calls=%async_computation.3 | async-start | bytes 16777216 | tf_op jit(solution)/shard_map/all_to_all | solution.py:117
  598.5 12.9 %copy-start.1 = (f32[1024,16,4,32]{0,1,3,2:T(8,128)S(1)}, f32[1024,16,4,32]{0,1,3,2:T(8,128)}, u32[]{:S(2)}) copy-start(f32[1024,16,4,32]{0,1,3,2:T(8,128)} %reshape.230) | copy-start | bytes 25165828
  793.4 29.8 %slice-start = ((s8[8388608]{0:T(1024)(128)(4,1)}), s8[4194304]{0:T(1024)(128)(4,1)S(1)}, s32[]{:S(2)}) async-start(s8[8388608]{0:T(1024)(128)(4,1)} %bitcast.181), calls=%async_computation.4 | async-start | bytes 8388608
  808.5 14.7 %slice-start.1 = ((s8[8388608]{0:T(1024)(128)(4,1)}), s8[4194304]{0:T(1024)(128)(4,1)S(1)}, s32[]{:S(2)}) async-start(s8[8388608]{0:T(1024)(128)(4,1)} %bitcast.181), calls=%async_computation.5 | async-start | bytes 8388608
  823.2 13.9 %copy-start.5 = (f32[1024,4,16,32]{0,3,2,1:T(8,128)S(1)}, f32[1024,4,16,32]{0,3,2,1:T(8,128)}, u32[]{:S(2)}) copy-start(f32[1024,4,16,32]{0,3,2,1:T(8,128)} %fusion.6) | copy-start | bytes 25165828
where the time goes:
time: 963 us; the launch traced here: 953 us
  waiting for transfers between devices  316 us (33%)
  matrix products  277 us (29%)
  local copies, waits for them, and re-layouts  212 us (22%)
  between operations  53.5 us (6%)
  blocking collectives  43.8 us (5%)
  starting transfers between devices  28.5 us (3%)
  other arithmetic  23 us (2%)
    all_to_all x1, waiting for transfers between devices, on_device(): lax.all_to_all(rotated_state[1].reshape(row_count, col_parts, GATE * low_...  136 us
    all_to_all x1, waiting for transfers between devices, on_device(): lax.all_to_all(rotated_state[0].reshape(row_count, col_parts, GATE * low_...  117 us
    dot_general x12, matrix products, complex_blend(): jnp.einsum(pattern, left_imag, right_real, precision=highest)  74.6 us
    dot_general x12, matrix products, complex_blend(): jnp.einsum(pattern, left_real, right_imag, precision=highest)  72.1 us
    dot_general x12, matrix products, complex_blend(): jnp.einsum(pattern, left_real, right_real, precision=highest)  66.3 us
    dot_general x12, matrix products, complex_blend(): jnp.einsum(pattern, left_imag, right_imag, precision=highest)  63.6 us
    all_to_all x1, waiting for transfers between devices, on_device(): lax.all_to_all(rho_imag.reshape(row_parts, GATE, low_width * col_count),...  53 us
    psum x1, blocking collectives, on_device(): lax.psum((part_trace_real, part_trace_imag, part_squares), ('row', 'col'))  43.8 us
  transfers between devices with their start and end apart: 4, of which 4 were waited for; matrix products, arithmetic and copies ran while one was open for 19% of the time, Pallas kernels for 0%

commit v1 on v0

--- a/solution.py
+++ b/solution.py
@@ -1,6 +1,10 @@
+import functools
+
 import jax
 import jax.numpy as jnp
 from jax import lax
+from jax.experimental import pallas as pl
+from jax.experimental.pallas import tpu as pltpu
 from jax.sharding import PartitionSpec as P
 
 LQ = 5
@@ -168,9 +172,208 @@
     return (mixed_real, depolarized_quadrature, purity)
 
 
+def gather_blocks(shape, real, imag, out, send_sem, recv_sem):
+    row_size, col_size, row_parts, col_parts, low_width = shape
+    devices = row_size * col_size
+    row = lax.axis_index("row")
+    col = lax.axis_index("col")
+    high = row_parts * low_width
+    wide = col_parts * low_width
+    stride = GATE * low_width
+
+    def partner(step):
+        place = lax.rem(row * col_size + col + step, devices)
+        return place // col_size, lax.rem(place, col_size)
+
+    def chunks(to_row, to_col):
+        for row_step in range(row_parts):
+            for col_step in range(col_parts):
+                for member, source in enumerate((real, imag)):
+                    yield (
+                        source.at[
+                            pl.ds(pl.multiple_of(row_step * stride + to_row * high, 8), high),
+                            pl.ds(pl.multiple_of(col_step * stride + to_col * wide, 128), wide),
+                        ],
+                        out.at[
+                            member * GATE + row * row_parts + row_step,
+                            :,
+                            pl.ds(
+                                pl.multiple_of((col * col_parts + col_step) * wide, 128), wide
+                            ),
+                        ],
+                    )
+
+    def start_step(step, carry):
+        to_row, to_col = partner(step)
+        for source, target in chunks(to_row, to_col):
+            pltpu.make_async_remote_copy(
+                src_ref=source,
+                dst_ref=target,
+                send_sem=send_sem,
+                recv_sem=recv_sem,
+                device_id=(to_row, to_col),
+                device_id_type=pl.DeviceIdType.MESH,
+            ).start()
+        return carry
+
+    lax.fori_loop(1, devices, start_step, 0)
+    for source, target in chunks(row, col):
+        pltpu.make_async_copy(source, target, recv_sem).start()
+    sent = out.at[pl.ds(0, 2 * GATE - 2 * GATE // devices)]
+    pltpu.make_async_copy(sent, sent, send_sem).wait()
+    pltpu.make_async_copy(out, out, recv_sem).wait()
+
+
+def split_weights(values):
+    high = lax.reduce_precision(values, 8, 7)
+    low = lax.reduce_precision(values - high, 8, 7)
+    return high.astype(jnp.bfloat16), low.astype(jnp.bfloat16)
+
+
+def split(values):
+    high = values.astype(jnp.bfloat16)
+    return high, (values - high.astype(jnp.float32)).astype(jnp.bfloat16)
+
+
+def dot(left, right):
+    def one(a, b):
+        return jnp.dot(a, b, preferred_element_type=jnp.float32)
+
+    return one(left[0], right[0]) + (one(left[0], right[1]) + one(left[1], right[0]))
+
+
+def rotate_blocks(shift_ref, held, left_high, left_low, right_high, right_low, real, imag):
+    size = real.shape[0]
+    row_step = pl.program_id(0)
+    col_step = pl.program_id(1)
+    low_width = size // GATE
+    wide = held.shape[-1] // GATE
+
+    def spread(lane):
+        pieces = []
+        for member in range(2):
+            state = held[member, :, 0].reshape(size, held.shape[-1])
+            for part in range(GATE):
+                start = part * wide + lane * low_width
+                pieces.append(state[:, start : start + low_width])
+        return jnp.concatenate(pieces, axis=1)
+
+    def finish(lane):
+        state = spread(lane)
+        middle = dot(split(state), (right_high[...], right_low[...]))
+        stacked = jnp.concatenate([middle[:, :size], middle[:, size:]], axis=0)
+        final = dot((left_high[...], left_low[...]), split(stacked))
+        rows = shift_ref[2].astype(jnp.int32)
+        cols = shift_ref[3].astype(jnp.int32)
+        on_diagonal = (
+            rows + row_step * size + lax.broadcasted_iota(jnp.int32, (size, size), 0)
+        ) == (cols + col_step * size + lax.broadcasted_iota(jnp.int32, (size, size), 1))
+        keep_share = 1 - mixing
+        zero = jnp.zeros((size, size), jnp.float32)
+        real[...] = keep_share * final[:size] + jnp.where(on_diagonal, shift_ref[0], zero)
+        imag[...] = keep_share * final[size:] + jnp.where(on_diagonal, shift_ref[1], zero)
+
+    for lane in range(wide // low_width):
+        pl.when(col_step == lane)(functools.partial(finish, lane))
+
+
+def direct(rho_real, rho_imag, gate_real_matrix, gate_imaginary, angles, targets, gate_order):
+    row_count, col_count = rho_real.shape
+    low_width = 2**LQ
+    row_size = lax.axis_size("row")
+    col_size = lax.axis_size("col")
+    row_parts = GATE // row_size
+    col_parts = GATE // col_size
+    size = GATE * low_width
+    high = row_parts * low_width
+    wide = col_parts * low_width
+    row_start = lax.axis_index("row") * row_count
+    col_start = lax.axis_index("col") * col_count
+    diagonal = (row_start + lax.broadcasted_iota(jnp.int32, (row_count, col_count), 0)) == (
+        col_start + lax.broadcasted_iota(jnp.int32, (row_count, col_count), 1)
+    )
+    zero = jnp.zeros_like(rho_real)
+    trace_real, trace_imag, squares = lax.psum(
+        (
+            jnp.sum(jnp.where(diagonal, rho_real, zero)),
+            jnp.sum(jnp.where(diagonal, rho_imag, zero)),
+            jnp.sum(rho_real * rho_real + rho_imag * rho_imag),
+        ),
+        ("row", "col"),
+    )
+    held = pl.pallas_call(
+        functools.partial(
+            gather_blocks, (row_size, col_size, row_parts, col_parts, low_width)
+        ),
+        out_shape=jax.ShapeDtypeStruct((2 * GATE, high, GATE * wide), jnp.float32),
+        in_specs=[pl.BlockSpec(memory_space=pl.ANY)] * 2,
+        out_specs=pl.BlockSpec(memory_space=pl.ANY),
+        scratch_shapes=[
+            pltpu.SemaphoreType.DMA,
+            pltpu.SemaphoreType.DMA,
+        ],
+        compiler_params=pltpu.CompilerParams(has_side_effects=True),
+    )(rho_real, rho_imag)
+    local_real, local_imag = joined_gate(angles, targets, gate_order, low_width)
+
+    def kron(first, second):
+        return (first[:, None, :, None] * second[None, :, None, :]).reshape(size, size)
+
+    whole_real = kron(gate_real_matrix, local_real) - kron(gate_imaginary, local_imag)
+    whole_imag = kron(gate_real_matrix, local_imag) + kron(gate_imaginary, local_real)
+    left = jnp.block([[whole_real, -whole_imag], [whole_imag, whole_real]])
+    right = jnp.block([[whole_real.T, -whole_imag.T], [whole_imag.T, whole_real.T]])
+    shift = jnp.stack(
+        [
+            mixing * trace_real / DIM,
+            mixing * trace_imag / DIM,
+            row_start.astype(jnp.float32),
+            col_start.astype(jnp.float32),
+        ]
+    )
+    full = pl.BlockSpec((2 * size, 2 * size), lambda i, j: (0, 0))
+    block = pl.BlockSpec((size, size), lambda i, j: (i, j))
+    mixed_real, depolarized_quadrature = pl.pallas_call(
+        rotate_blocks,
+        grid=(row_parts, col_parts),
+        out_shape=[jax.ShapeDtypeStruct((row_count, col_count), jnp.float32)] * 2,
+        in_specs=[
+            pl.BlockSpec(memory_space=pltpu.SMEM),
+            pl.BlockSpec(
+                (2, GATE, 1, low_width, GATE * wide), lambda i, j: (0, 0, i, 0, 0)
+            ),
+            full,
+            full,
+            full,
+            full,
+        ],
+        out_specs=[block, block],
+        compiler_params=pltpu.CompilerParams(vmem_limit_bytes=60 * 2**20),
+    )(
+        shift,
+        held.reshape(2, GATE, row_parts, low_width, GATE * wide),
+        *split_weights(left),
+        *split_weights(right),
+    )
+    keep_share = 1 - mixing
+    trace_squared = trace_real * trace_real + trace_imag * trace_imag
+    purity = (
+        keep_share * keep_share * squares
+        + (2 * keep_share * mixing + mixing * mixing) * trace_squared / DIM
+    ) / (DIM * DIM)
+    return (mixed_real, depolarized_quadrature, purity)
+
+
 def solution(mesh):
     in_specs = (P("row", "col"), P("row", "col"), P(), P(), P(), P(), P())
     out_specs = (P("row", "col"), P("row", "col"), P())
+    col_parts = GATE // mesh.shape["col"]
+    row_parts = GATE // mesh.shape["row"]
+    aligned = col_parts * 2**LQ % 128 == 0 and mesh.shape["col"] == 4 and row_parts == 2
     return jax.shard_map(
-        on_device, mesh=mesh, in_specs=in_specs, out_specs=out_specs, check_vma=False
-    )
+        direct if aligned else on_device,
+        mesh=mesh,
+        in_specs=in_specs,
+        out_specs=out_specs,
+        check_vma=False,
+    )

time: 963 us -> 592 us (0.61)
  Pallas kernels: 0 us -> 440 us
  waiting for transfers between devices: 316 us -> 0 us
  matrix products: 277 us -> 6.77 us
  local copies, waits for them, and re-layouts: 212 us -> 19.7 us
  starting transfers between devices: 28.5 us -> 0 us
    pallas_call x0 -> x2, Pallas kernels: none -> 440 us  [the longest x1 370 us: direct(): pl.pallas_call(functools.partial(gather_blocks, (row_size, col_size, row_...]
    all_to_all x4 -> x0, waiting for transfers between devices: 316 us -> none  [the longest x1 136 us: on_device(): lax.all_to_all(rotated_state[1].reshape(row_count, col_parts, GATE * low_...]
    reshape x12 -> x0, local copies, waits for them, and re-layouts: 140 us -> none  [the longest x2 22.9 us: on_device(): rho_real.reshape(row_parts, GATE, low_width * col_count)]
    dot_general x12 -> x8, matrix products: 74.6 us -> 1.7 us  [complex_blend(): jnp.einsum(pattern, left_imag, right_real, precision=highest)]
    dot_general x12 -> x8, matrix products: 72.1 us -> 1.66 us  [complex_blend(): jnp.einsum(pattern, left_real, right_imag, precision=highest)]
    dot_general x12 -> x8, matrix products: 66.3 us -> 1.68 us  [complex_blend(): jnp.einsum(pattern, left_real, right_real, precision=highest)]
    dot_general x12 -> x8, matrix products: 63.6 us -> 1.73 us  [complex_blend(): jnp.einsum(pattern, left_imag, right_imag, precision=highest)]
    all_to_all x4 -> x0, local copies, waits for them, and re-layouts: 50.2 us -> none  [the longest x1 15.3 us: on_device(): lax.all_to_all(rho_real.reshape(row_parts, GATE, low_width * col_count),...]
  transfers between devices with their start and end apart: 4 -> 0, of which waited for: 4 -> 0; matrix products, arithmetic and copies ran while one was open for 19% -> 0% of each run, Pallas kernels for 0% -> 0%
where the time goes in v1:
time: 592 us; the launch traced here: 591 us
  Pallas kernels  440 us (74%)
  between operations  51.7 us (9%)
  blocking collectives  40.9 us (7%)
  other arithmetic  31.8 us (5%)
  local copies, waits for them, and re-layouts  19.7 us (3%)
  matrix products  6.77 us (1%)
    pallas_call x1, Pallas kernels, direct(): pl.pallas_call(functools.partial(gather_blocks, (row_size, col_size, row_...  370 us
    pallas_call x1, Pallas kernels, direct(): pl.pallas_call(rotate_blocks, grid=(row_parts, col_parts), out_shape=[jax...  70 us
    psum x1, blocking collectives, direct(): lax.psum((jnp.sum(jnp.where(diagonal, rho_real, zero)), jnp.sum(jnp.where...  40.9 us

profile of v1, /device:TPU:14, one launch (start us, length us, event | category | flops | bytes accessed | tf_op | source)
XLA Modules:
  0.0 590.7 jit_solution(12950230513787530093)
XLA Ops:
  0.6 1.6 fusion.190
  2.3 0.7 iota_compare_fusion.4
  2.9 0.7 iota_compare_fusion.5
  3.6 0.6 iota_compare_fusion.6
  4.2 0.6 iota_compare_fusion.7
  4.8 0.6 iota_compare_fusion.8
  5.5 0.6 iota_compare_fusion.9
  6.1 0.6 iota_compare_fusion.10
  6.7 0.6 iota_compare_fusion.3
  7.3 6.4 %select_reduce_fusion.15 = (s32[]{:T(128)}, s32[]{:T(128)}, s32[]{:T(128)}, s32[]{:T(128)}, s32[]{:T(128)}, /*index=5*/s32[]{:T(128)}, s32[]{:T(128)}, s32[]{:T(128)}) fusion(s32[8]{0:T(128)} %param.12, s32[]{:T(128)} %bitcast.5, s32[]{:T(128)} %bitcast.30, s32[]{:T(128)} %bitcast.25, s32[]{:T(128)} %bitcast.20, s32[]{:T(128)} %bitcast.15, s32[]{:T(128)} %bitcast.10, ...), kind=kLoop, calls=%fused_computation.236 | loop fusion | flops 184 | bytes 96 | tf_op jit(solution)/shard_map/reduce_sum | solution.py:69
  18.7 0.9 select_reduce_fusion.7
  19.7 0.7 fusion.182
  30.5 0.7 fusion.186
  41.3 0.7 fusion.184
  52.1 0.7 fusion.188
  63.0 8.0 %add_reduce_fusion = (f32[]{:T(128)}, f32[]{:T(128)}, f32[]{:T(128)}) fusion(f32[1024,2048]{1,0:T(8,128)} %imag.1, f32[1024,2048]{1,0:T(8,128)} %real.1, s32[2048]{0:T(1024)S(1)} %iota_add_fusion, s32[1024]{0:T(1024)S(1)} %iota_add_fusion.1), kind=kLoop, calls=%fused_computation.4 | loop fusion | flops 18874364 | bytes 16789516 | tf_op jit(solution)/shard_map/reduce_sum | solution.py:300
  71.0 40.9 %all-reduce = (f32[]{:T(128)}, f32[]{:T(128)}, f32[]{:T(128)}) all-reduce(f32[]{:T(128)} %get-tuple-element.9, f32[]{:T(128)} %get-tuple-element.8, f32[]{:T(128)} %get-tuple-element.7), channel_id=1, replica_groups=mesh['row'=8,'col'=4] {'row','col'}, use_global_device_ids=true, to_apply=%region_3.4 | all-reduce | flops 3 | bytes 24 | tf_op jit(solution)/shard_map/psum | solution.py:296
  116.4 0.6 pad_maximum_fusion.shift_ref
  117.0 0.1 copy.10
  117.1 0.2 fusion.7
  117.3 0.2 convolution_add_fusion.7
  117.5 0.2 fusion.6
  117.7 0.2 convolution_subtract_fusion.7
  118.0 0.2 fusion.9
  118.2 0.2 convolution_subtract_fusion.6
  118.4 0.2 fusion.8
  118.6 0.2 convolution_add_fusion.6
  118.8 0.2 fusion.10
  119.0 0.2 convolution_add_fusion.5
  119.3 0.2 fusion.11
  119.5 0.2 convolution_subtract_fusion.5
  119.7 0.2 fusion.13
  119.9 0.2 convolution_subtract_fusion.4
  120.1 0.2 fusion.12
  120.3 0.2 convolution_add_fusion.4
  120.5 0.2 fusion.14
  120.8 0.2 convolution_add_fusion.3
  121.0 0.2 fusion.15
  121.2 0.2 convolution_subtract_fusion.3
  121.4 0.2 fusion.17
  121.6 0.2 convolution_subtract_fusion.2
  121.8 0.2 fusion.16
  122.0 0.2 convolution_add_fusion.2
  122.3 0.2 fusion.18
  122.5 0.2 convolution_add_fusion.1
  122.7 0.2 fusion.19
  122.9 0.2 convolution_subtract_fusion.1
  123.1 0.2 fusion.21
  123.3 0.2 convolution_subtract_fusion
  123.6 0.2 fusion.20
  123.8 0.2 convolution_add_fusion
  124.0 0.1 copy.13
  124.1 0.1 copy.11
  124.1 4.6 multiply_add_fusion
  128.8 3.5 add.120
  132.3 3.6 sub.45
  135.9 0.1 bitcast_negate_fusion
  136.0 0.1 neg.86
  136.1 2.9 fusion.3
  139.0 4.0 copy.15.left_low
  142.9 4.0 copy.14.left_high
  146.9 2.9 fusion.5
  149.8 369.9 %shard_map.94 = f32[32,64,2048]{2,1,0:T(8,128)} custom-call(f32[1024,2048]{1,0:T(8,128)} %real.1, f32[1024,2048]{1,0:T(8,128)} %imag.1), custom_call_target="tpu_custom_call" | custom-call | tf_op jit(solution)/shard_map/pallas_call | solution.py:304
  519.6 70.0 %shard_map.95 = (f32[1024,2048]{1,0:T(8,128)}, f32[1024,2048]{1,0:T(8,128)}) custom-call(f32[4]{0:T(128)} %pad_maximum_fusion.shift_ref, f32[2,16,2,32,2048]{4,3,2,1,0:T(8,128)} %bitcast.108, bf16[1024,1024]{1,0:T(8,128)(2,1)} %copy.14.left_high, bf16[1024,1024]{1,0:T(8,128)(2,1)} %copy.15.left_low, bf16[1024,1024]{1,0:T(8,128)(2,1)} %get-tuple-element.30.right_high, ...), custom_call_target="tpu_custom_call" | custom-call | tf_op jit(solution)/shard_map/pallas_call | solution.py:336
  (47 shorter events, 0.4 us)
Async XLA Ops:
  63.0 54.0 %copy-start = (f32[16,16]{1,0:T(8,128)S(1)}, f32[16,16]{1,0:T(8,128)}, u32[]{:S(2)}) copy-start(f32[16,16]{1,0:T(8,128)} %param.9) | copy-start | bytes 3076
  63.0 54.1 %copy-start.1 = (f32[16,16]{1,0:T(8,128)S(1)}, f32[16,16]{1,0:T(8,128)}, u32[]{:S(2)}) copy-start(f32[16,16]{1,0:T(8,128)} %param.10) | copy-start | bytes 3076
